TPU v7x, 256 devices: a whole 4x4x8 slice. The times are simulated.
256 devices in a mesh: ctx: 128 (over x, y_hi, z, core), head: 2 (over y_lo).
Axes of the slice: x: 4, y: 4 (y_hi: 2, y_lo: 2; y = y_hi * 2 + y_lo), z: 8, core: 2. Of those that a mesh axis runs over, the one named last changes fastest.
Arguments:
- queries: bfloat16 [16384, 2048], P('ctx', 'head'), may hold values from -160 to 160
- rotated_keys: bfloat16 [16384, 512], P('ctx', 'head'), may hold values from -6 to 6
- value_matrix: bfloat16 [16384, 512], P('ctx', 'head'), may hold values from -6 to 6
- doc_lengths: int32 [8], replicated, may hold values from 1 to 12288, 16384 in all
- scored: int32 [512], P('ctx'), may hold values from 0 to 127, as said below
- residual: bfloat16 [512, 4096], P('ctx', 'head'), may hold values from -18 to 18
- norm_gain: float32 [4096], P('head'), may hold values from 0.5 to 1.5
- out_weight: bfloat16 [2048, 4096], P('head'), may hold values from -0.5 to 0.5
- lm_weight: bfloat16 [4096, 128256], P('head', 'ctx'), may hold values from -0.40625 to 0.40625
- token_ids: int32 [512], replicated, may hold values from 0 to 128255
- old_logp: float32 [512], replicated, may hold values from -24 to -9
- advantage: float32 [512], replicated, may hold values from -3 to 3
Outputs:
- attended: bfloat16 [16384, 2048], P('ctx', 'head')
- log_probs: float32 [512], replicated
- token_loss: float32 [512], replicated
Inputs may be any that keep to these rules, and one draw needn't show every extreme that they name: `scored`: each aligned block of 4 entries holds distinct increasing offsets. `doc_lengths`: the longest document has exactly three quarters of 16384 positions.
All inputs are finite; a program needn't handle non-finite values.
Results may differ from a plain program's by a relative error of at most 0.0065.
Values may be sent and summed in bfloat16 or wider, within the bound.
A program may use at most 128 MiB of HBM per device.

v0:
```python
import math
import jax
import jax.numpy as jnp
from jax import lax
from jax.sharding import Mesh
from jax.sharding import PartitionSpec as P

HEAD_SIZE = 128
CTX = ("ctx_0", "ctx_1", "ctx_2", "ctx_3")
CTX_HEAD = ("ctx_0", "ctx_1", "ctx_2", "ctx_3", "head")
masked_score = -1e30


def side_by_side(arrays, axis, dim, along):
    both = jnp.concatenate(arrays, axis=along)
    whole, at, outs = (lax.all_gather(both, axis, axis=dim, tiled=True), 0, [])
    for a in arrays:
        outs.append(lax.slice_in_dim(whole, at, at + a.shape[along], axis=along))
        at += a.shape[along]
    return tuple(outs)


def in_blocks(shard, dim, peers):
    before, after = (shard.shape[:dim], shard.shape[dim + 1 :])
    return jnp.moveaxis(shard.reshape(*before, peers, -1, *after), dim, 0)


def sum_at_owner(shard, axis, dim):
    pieces = in_blocks(shard, dim, lax.axis_size(axis))
    arrived = lax.all_to_all(pieces, axis, split_axis=0, concat_axis=0, tiled=True)
    return arrived.astype(jnp.float32).sum(axis=0)


def sent_to_all(shard, axis):
    peers = lax.axis_size(axis)
    return lax.all_to_all(
        jnp.broadcast_to(shard[None], (peers, *shard.shape)), axis, 0, 0, tiled=True
    )


def of_everyone(shard, axis):
    everything = sent_to_all(shard, axis)
    return jnp.sum(everything, axis=0)


def all_in_one(shard, axis):
    leaves = jax.tree.leaves(shard)
    order = sorted(range(len(leaves)), key=lambda k: -leaves[k].size)
    width = (1, *leaves[order[0]].shape)[-1]
    lines = [
        jnp.pad(leaves[k].reshape(-1), (0, -leaves[k].size % width)).reshape(-1, width)
        for k in order
    ]
    both, at, found = (lax.all_gather(jnp.concatenate(lines), axis), 0, {})
    for k, line in zip(order, lines):
        slab = both[:, at : at + len(line)].reshape(len(both), -1)
        found[k] = slab[:, : leaves[k].size].reshape(-1, *leaves[k].shape)
        at += len(line)
    numbers = iter(range(len(leaves)))
    return jax.tree.map(lambda _: found[next(numbers)], shard)


def merged_by_axis(shard, axes, combine):
    for axis in axes:
        pieces = all_in_one(shard, axis)
        shard = jax.tree.map(lambda part: part[0], pieces)
        for k in range(1, lax.axis_size(axis)):
            shard = combine(shard, jax.tree.map(lambda part: part[k], pieces))
    return shard


def doc_index(positions, doc_ends):
    return jnp.sum((positions[:, None] >= doc_ends[None, :]).astype(jnp.int32), axis=1)


def attend_rows(running, context, key_part, value_part, offset):
    query_heads, query_pos, query_doc, doc_ends, first_start, skipping = context
    row_top, row_total, accumulated = running
    row_count = key_part.shape[0]
    kv_heads = query_heads.shape[1]
    key_head_rows = key_part.reshape(row_count, kv_heads, HEAD_SIZE)
    value_head_rows = value_part.reshape(row_count, kv_heads, HEAD_SIZE)
    scores = jnp.einsum(
        "qkgd,rkd->kgqr", query_heads, key_head_rows, preferred_element_type=jnp.float32
    ) * HEAD_SIZE ** (-0.5)
    key_pos = offset + jnp.arange(row_count, dtype=jnp.int32)
    allowed = (
        (key_pos[None, :] <= query_pos[:, None])
        & (key_pos[None, :] >= 0)
        & (doc_index(key_pos, doc_ends)[None, :] == query_doc[:, None])
    )
    scores = jnp.where(allowed, scores, masked_score)
    new_top = jnp.maximum(row_top, jnp.max(scores, axis=-1))
    weights = jnp.where(allowed, jnp.exp(scores - new_top[..., None]), 0.0)
    rescale = jnp.exp(row_top - new_top)
    row_total = row_total * rescale + jnp.sum(weights, axis=-1)
    update = jnp.einsum(
        "kgqr,rkd->kgqd",
        weights.astype(jnp.bfloat16),
        value_head_rows,
        preferred_element_type=jnp.float32,
    )
    accumulated = accumulated * rescale[..., None] + update
    return (new_top, row_total, accumulated)


def attend_piece(running, shard_piece, context):
    key_rows, value_rows = shard_piece
    row_count = key_rows.shape[0]
    block_rows = math.gcd(row_count, 512)
    block_count = row_count // block_rows

    def one_block(block_index, carried):
        start_row = block_index * block_rows
        key_part = lax.dynamic_slice_in_dim(key_rows, start_row, block_rows, 0)
        value_part = lax.dynamic_slice_in_dim(value_rows, start_row, block_rows, 0)
        return attend_rows(carried, context, key_part, value_part, start_row)

    return lax.fori_loop(0, block_count, one_block, running)


def combine(earlier, later):
    top_one, sum_one, target_one = earlier
    top_two, sum_two, target_two = later
    new_top = jnp.maximum(top_one, top_two)
    merged_sum = sum_one * jnp.exp(top_one - new_top) + sum_two * jnp.exp(top_two - new_top)
    return (new_top, merged_sum, target_one + target_two)


def per_device(
    queries,
    rotated_keys,
    value_matrix,
    doc_lengths,
    scored,
    residual,
    norm_gain,
    out_weight,
    lm_weight,
    token_ids,
    old_logp,
    advantage,
):
    tok_rows = queries.shape[0]
    kv_heads = rotated_keys.shape[1] // HEAD_SIZE
    group_count = queries.shape[1] // rotated_keys.shape[1]
    my_index = lax.axis_index(CTX)
    doc_ends = jnp.cumsum(doc_lengths)
    doc_starts = doc_ends - doc_lengths
    query_pos = my_index * tok_rows + jnp.arange(tok_rows, dtype=jnp.int32)
    query_doc = doc_index(query_pos, doc_ends)
    first_start = jnp.max(jnp.where(doc_starts <= query_pos[0], doc_starts, 0))
    query_heads = queries.reshape(tok_rows, kv_heads, group_count, HEAD_SIZE)
    context = (query_heads, query_pos, query_doc, doc_ends, first_start, False)
    state_shape = (kv_heads, group_count, tok_rows)
    initial = (
        jnp.full(state_shape, masked_score, jnp.float32),
        jnp.zeros(state_shape, jnp.float32),
        jnp.zeros(state_shape + (HEAD_SIZE,), jnp.float32),
    )
    row_top, row_total, accumulated = attend_piece(
        initial, side_by_side((rotated_keys, value_matrix), CTX, 0, 1), context
    )
    result = accumulated / row_total[..., None]
    attended = (
        jnp.transpose(result, (2, 0, 1, 3))
        .reshape(tok_rows, kv_heads * group_count * HEAD_SIZE)
        .astype(jnp.bfloat16)
    )
    chosen = jnp.take(attended, scored, axis=0)
    partial_value = jnp.dot(chosen, out_weight, preferred_element_type=jnp.float32)
    projected = sum_at_owner(partial_value.astype(jnp.bfloat16), "head", 1)
    hidden = residual.astype(jnp.float32) + projected
    squares = of_everyone(jnp.sum(hidden * hidden, axis=1), "head")
    full_width = hidden.shape[1] * lax.axis_size("head")
    normed = (
        hidden * lax.rsqrt(squares[:, None] / full_width + 1e-05) * norm_gain[None, :]
    ).astype(jnp.bfloat16)
    partial_logits = jnp.dot(
        lax.all_gather(normed, CTX, axis=0, tiled=True),
        lm_weight,
        preferred_element_type=jnp.float32,
    )
    logits = sum_at_owner(partial_logits.astype(jnp.bfloat16), "head", 1)
    vocab_rows = logits.shape[1]
    vocab_start = (
        my_index * vocab_rows * lax.axis_size("head") + lax.axis_index("head") * vocab_rows
    )
    local_ids = token_ids - vocab_start
    matches = local_ids[:, None] == jnp.arange(vocab_rows, dtype=jnp.int32)[None, :]
    target_part = jnp.sum(jnp.where(matches, logits, 0.0), axis=1)
    local_top = jnp.max(logits, axis=1)
    sum_part = jnp.sum(jnp.exp(logits - local_top[:, None]), axis=1)
    global_top, exp_total, target = merged_by_axis(
        (local_top, sum_part, target_part), CTX_HEAD, combine
    )
    log_probs = target - global_top - jnp.log(exp_total)
    ratio = jnp.exp(jnp.clip(log_probs - old_logp, -4.0, 4.0))
    token_loss = -jnp.minimum(ratio * advantage, jnp.clip(ratio, 0.8, 1.2) * advantage)
    return (attended, log_probs, token_loss)


def solution(mesh):
    finer = Mesh(
        mesh.devices.reshape(4, 2, 8, 2, mesh.shape["head"]),
        ("ctx_0", "ctx_1", "ctx_2", "ctx_3", "head"),
    )
    placed = (
        P(CTX, "head"),
        P(CTX, "head"),
        P(CTX, "head"),
        P(),
        P(CTX),
        P(CTX, "head"),
        P("head"),
        P("head", None),
        P("head", CTX),
        P(),
        P(),
        P(),
    )
    return jax.shard_map(
        per_device,
        mesh=finer,
        in_specs=placed,
        out_specs=(P(CTX, "head"), P(), P()),
        check_vma=False,
    )
```

profile of v0, /device:TPU:1, one launch (start us, length us, event | category | flops | bytes accessed | tf_op | source)
XLA Modules:
  0.0 491.9 jit_solution(17511669347726125021)
XLA Ops:
  10.7 1.1 copy.48
  13.5 137.7 %all-gather.14.cloned.1.call-done = bf16[16384,512]{0,1:T(8,128)(2,1)} async-done(((bf16[128,512]{0,1:T(8,128)(2,1)}), bf16[16384,512]{0,1:T(8,128)(2,1)}) %all-gather.14.cloned.1.call-update) | async-done | bytes 16777232 | tf_op jit(solution)/shard_map/all_gather | solution.py:16
  151.2 11.4 %fusion.76 = (bf16[16384,256]{0,1:T(8,128)(2,1)}, bf16[16384,256]{0,1:T(8,128)(2,1)}) fusion(bf16[16384,512]{0,1:T(8,128)(2,1)} %all-gather.14.cloned.1.call-done), kind=kLoop, calls=%fused_computation.157 | loop fusion | bytes 33554432 | tf_op jit(solution)/shard_map/slice | solution.py:18
  162.7 113.7 %while.18 = (s32[]{:T(128)}, f32[2,4,128]{2,1,0:T(4,128)S(1)}, f32[2,4,128]{2,1,0:T(4,128)S(1)}, f32[2,4,128,128]{3,2,1,0:T(8,128)S(1)}, s32[8]{0:T(128)S(1)}, /...) while((s32[]{:T(128)}, f32[2,4,128]{2,1,0:T(4,128)S(1)}, ...), condition=%wide.region_6.7_spmd.clone, body=%wide.region_2.6_spmd.clone.sunk | while | flops 275925120 | bytes 9515759 | solution.py:119
  163.1 1.1 constant_dynamic-slice_fusion.3
  166.6 1.1 constant_dynamic-slice_fusion.3
  170.2 1.1 constant_dynamic-slice_fusion.3
  173.7 1.1 constant_dynamic-slice_fusion.3
  177.3 1.1 constant_dynamic-slice_fusion.3
  180.8 1.1 constant_dynamic-slice_fusion.3
  184.4 1.1 constant_dynamic-slice_fusion.3
  187.9 1.1 constant_dynamic-slice_fusion.3
  195.0 1.1 constant_dynamic-slice_fusion.3
  198.6 1.1 constant_dynamic-slice_fusion.3
  202.1 1.1 constant_dynamic-slice_fusion.3
  205.7 1.1 constant_dynamic-slice_fusion.3
  209.3 1.1 constant_dynamic-slice_fusion.3
  212.8 1.1 constant_dynamic-slice_fusion.3
  216.4 1.1 constant_dynamic-slice_fusion.3
  219.9 1.1 constant_dynamic-slice_fusion.3
  223.5 1.1 constant_dynamic-slice_fusion.3
  227.0 1.1 constant_dynamic-slice_fusion.3
  230.6 1.1 constant_dynamic-slice_fusion.3
  234.1 1.1 constant_dynamic-slice_fusion.3
  241.2 1.1 constant_dynamic-slice_fusion.3
  244.8 1.1 constant_dynamic-slice_fusion.3
  248.3 1.1 constant_dynamic-slice_fusion.3
  251.9 1.1 constant_dynamic-slice_fusion.3
  255.5 1.1 constant_dynamic-slice_fusion.3
  259.0 1.1 constant_dynamic-slice_fusion.3
  262.6 1.1 constant_dynamic-slice_fusion.3
  266.1 1.1 constant_dynamic-slice_fusion.3
  269.7 1.1 constant_dynamic-slice_fusion.3
  273.2 1.1 constant_dynamic-slice_fusion.3
  277.6 4.6 convolution_convert_fusion
  282.2 5.1 %all_to_all.16 = bf16[2,4,2048]{2,1,0:T(4,128)(2,1)S(1)} all-to-all(bf16[2,4,2048]{2,1,0:T(4,128)(2,1)S(1)} %bitcast.366), channel_id=1, replica_groups=mesh['ctx_0'=4,'ctx_1'=2,'ctx_2'=8,'ctx_3'=2,'head'=2] {'head'}, dimensions={0} | all-to-all | bytes 65536 | tf_op jit(solution)/shard_map/all_to_all | solution.py:30
  287.5 5.0 %all_to_all.17 = f32[2,1,4]{2,1,0:T(1,128)S(1)} all-to-all(f32[2,1,4]{2,1,0:T(1,128)S(1)} %broadcast_in_dim.94), channel_id=1, replica_groups=mesh['ctx_0'=4,'ctx_1'=2,'ctx_2'=8,'ctx_3'=2,'head'=2] {'head'}, dimensions={0} | all-to-all | bytes 64 | tf_op jit(solution)/shard_map/all_to_all | solution.py:36
  293.2 116.8 %all-gather.16.cloned.1.call-done = bf16[128,4,2048]{2,1,0:T(4,128)(2,1)} async-done(((bf16[1,4,2048]{2,1,0:T(4,128)(2,1)}), bf16[128,4,2048]{2,1,0:T(4,128)(2,1)}) %all-gather.16.cloned.1.call-update) | async-done | bytes 2097168 | tf_op jit(solution)/shard_map/all_gather | solution.py:180
  410.0 2.5 reshape.1099
  412.6 4.5 convolution_convert_fusion.1
  417.1 1.2 reshape.1077
  418.3 3.6 all-to-all-start.2
  421.9 13.2 %all-to-all-done.2 = bf16[2,512,501]{1,2,0:T(8,128)(2,1)S(1)} async-done(((bf16[2,512,501]{1,2,0:T(8,128)(2,1)}), bf16[2,512,501]{1,2,0:T(8,128)(2,1)S(1)}, u32[]{:S(2)}, u32[]{:S(2)}) %all-to-all-start.2) | async-done | bytes 1026080 | tf_op jit(solution)/shard_map/all_to_all | solution.py:30
  435.7 9.6 %all-gather.6 = f32[4,3,512]{2,1,0:T(4,128)S(1)} all-gather(f32[1,3,512]{2,1,0:T(4,128)S(1)} %maximum_bitcast_fusion), channel_id=2, replica_groups=mesh['ctx_0'=4,'ctx_1'=2,'ctx_2'=8,'ctx_3'=2,'head'=2] {'ctx_0'}, dimensions={0}, use_global_device_ids=true | all-gather | bytes 30720 | tf_op jit(solution)/shard_map/all_gather | solution.py:54
  445.3 4.7 all-gather.7
  450.1 18.4 %all-gather.8 = f32[8,3,512]{2,1,0:T(4,128)S(1)} all-gather(f32[1,3,512]{2,1,0:T(4,128)S(1)} %maximum_bitcast_fusion.2), channel_id=4, replica_groups=mesh['ctx_0'=4,'ctx_1'=2,'ctx_2'=8,'ctx_3'=2,'head'=2] {'ctx_2'}, dimensions={0}, use_global_device_ids=true | all-gather | bytes 55296 | tf_op jit(solution)/shard_map/all_gather | solution.py:54
  468.6 12.6 %all-gather.9 = f32[2,3,512]{2,1,0:T(4,128)S(1)} all-gather(f32[1,3,512]{2,1,0:T(4,128)S(1)} %maximum_bitcast_fusion.3), channel_id=5, replica_groups=mesh['ctx_0'=4,'ctx_1'=2,'ctx_2'=8,'ctx_3'=2,'head'=2] {'ctx_3'}, dimensions={0}, use_global_device_ids=true | all-gather | bytes 18432 | tf_op jit(solution)/shard_map/all_gather | solution.py:54
  481.2 3.2 all-gather.10
  (412 shorter events, 87.7 us)
Async XLA Ops:
  7.2 144.1 %all-gather.14.cloned.1.call-start = ((), (), s32[]{:S(2)}) async-start(), calls=%async_computation.3 | async-start | bytes 16908288 | tf_op jit(solution)/shard_map/all_gather | solution.py:16
  9.8 400.2 %all-gather.16.cloned.1.call-start = ((), (), s32[]{:S(2)}) async-start(), calls=%async_computation.4 | async-start | bytes 2113536 | tf_op jit(solution)/shard_map/all_gather | solution.py:180
  277.0 5.2 %copy-start = (bf16[128,1024]{1,0:T(8,128)(2,1)}, bf16[128,1024]{1,0:T(8,128)(2,1)S(1)}, u32[]{:S(2)}) copy-start(bf16[128,1024]{1,0:T(8,128)(2,1)S(1)} %convert_element_type.47) | copy-start | bytes 786436
  277.6 9.8 %copy-start.1 = (bf16[4,2048]{1,0:T(4,128)(2,1)S(1)}, bf16[4,2048]{1,0:T(4,128)(2,1)}, u32[]{:S(2)}) copy-start(bf16[4,2048]{1,0:T(4,128)(2,1)} %param.19) | copy-start | bytes 49156
  277.6 14.9 %copy-start.2 = (f32[2048]{0:T(1024)S(1)}, f32[2048]{0:T(1024)}, u32[]{:S(2)}) copy-start(f32[2048]{0:T(1024)} %param.20) | copy-start | bytes 24580
  417.1 4.8 copy-start.5
  418.3 16.8 %all-to-all-start.2 = ((bf16[2,512,501]{1,2,0:T(8,128)(2,1)}), bf16[2,512,501]{1,2,0:T(8,128)(2,1)S(1)}, u32[]{:S(2)}, u32[]{:S(2)}) async-start(bf16[2,512,501]{1,2,0:T(8,128)(2,1)} %bitcast.8), calls=%async_computation.2 | async-start | bytes 2064384 | tf_op jit(solution)/shard_map/all_to_all | solution.py:30
  421.9 62.6 %copy-start.3 = (f32[512]{0:T(512)S(1)}, f32[512]{0:T(512)}, u32[]{:S(2)}) copy-start(f32[512]{0:T(512)} %param.25) | copy-start | bytes 6148
  421.9 62.6 %copy-start.4 = (f32[512]{0:T(512)S(1)}, f32[512]{0:T(512)}, u32[]{:S(2)}) copy-start(f32[512]{0:T(512)} %param.24) | copy-start | bytes 6148
Sparse Core Ops, SparseCore 0:
  12.3 138.8 all-gather.13
  293.3 116.6 all-gather.15
where the time goes:
time: 493 us; the launch traced here: 492 us
  waiting for transfers between devices  268 us (54%)
  blocking collectives  58.6 us (12%)
  matrix products  56.6 us (11%)
  local copies, waits for them, and re-layouts  53.7 us (11%)
  other arithmetic  34.8 us (7%)
  between operations  14.4 us (3%)
    all_gather x1, waiting for transfers between devices, side_by_side(): whole, at, outs = (lax.all_gather(both, axis, axis=dim, tiled=True), 0, [])  138 us
    all_gather x1, waiting for transfers between devices, per_device(): lax.all_gather(normed, CTX, axis=0, tiled=True)  117 us
    all_gather x5, blocking collectives, all_in_one(): both, at, found = (lax.all_gather(jnp.concatenate(lines), axis), 0, {})  48.5 us
    dynamic_slice x32, local copies, waits for them, and re-layouts, one_block(): value_part = lax.dynamic_slice_in_dim(value_rows, start_row, block_rows, 0)  34.3 us
    dot_general x32, matrix products, attend_rows(): jnp.einsum('kgqr,rkd->kgqd', weights.astype(jnp.bfloat16), value_head_row...  30.3 us
    dot_general x32, matrix products, attend_rows(): jnp.einsum('qkgd,rkd->kgqr', query_heads, key_head_rows, preferred_elemen...  17.2 us
    reduce_sum x32, other arithmetic, attend_rows(): row_total = row_total * rescale + jnp.sum(weights, axis=-1)  16.7 us
    all_to_all x1, waiting for transfers between devices, sum_at_owner(): lax.all_to_all(pieces, axis, split_axis=0, concat_axis=0, tiled=True)  13.2 us
  transfers between devices with their start and end apart: 3, of which 3 were waited for; matrix products, arithmetic and copies ran while one was open for 1% of the time, Pallas kernels for 0%

commit v1 on v0

--- a/solution.py
+++ b/solution.py
@@ -9,6 +9,13 @@
 CTX = ("ctx_0", "ctx_1", "ctx_2", "ctx_3")
 CTX_HEAD = ("ctx_0", "ctx_1", "ctx_2", "ctx_3", "head")
 masked_score = -1e30
+
+
+def gather_over(value, name, dim):
+    size = lax.axis_size(name)
+    blocks = jnp.stack([value for _ in range(size)])
+    blocks = lax.all_to_all(blocks, name, split_axis=0, concat_axis=0)
+    return jnp.concatenate(blocks, axis=dim)
 
 
 def side_by_side(arrays, axis, dim, along):
@@ -177,9 +184,7 @@
         hidden * lax.rsqrt(squares[:, None] / full_width + 1e-05) * norm_gain[None, :]
     ).astype(jnp.bfloat16)
     partial_logits = jnp.dot(
-        lax.all_gather(normed, CTX, axis=0, tiled=True),
-        lm_weight,
-        preferred_element_type=jnp.float32,
+        gather_over(normed, CTX, 0), lm_weight, preferred_element_type=jnp.float32
     )
     logits = sum_at_owner(partial_logits.astype(jnp.bfloat16), "head", 1)
     vocab_rows = logits.shape[1]

time: 493 us -> 442 us (0.90)
  waiting for transfers between devices: 268 us -> 149 us
  blocking collectives: 58.6 us -> 125 us
    all_gather x1 -> x0, waiting for transfers between devices: 117 us -> none  [per_device(): lax.all_gather(normed, CTX, axis=0, tiled=True)]
    all_to_all x0 -> x1, blocking collectives: none -> 64.7 us  [gather_over(): blocks = lax.all_to_all(blocks, name, split_axis=0, concat_axis=0)]
  transfers between devices with their start and end apart: 3 -> 2, of which waited for: 3 -> 2; matrix products, arithmetic and copies ran while one was open for 1% -> 1% of each run, Pallas kernels for 0% -> 0%
where the time goes in v1:
time: 442 us; the launch traced here: 441 us
  waiting for transfers between devices  149 us (34%)
  blocking collectives  125 us (28%)
  matrix products  57.3 us (13%)
  local copies, waits for them, and re-layouts  54.3 us (12%)
  other arithmetic  34.2 us (8%)
  between operations  14.4 us (3%)
    all_gather x1, waiting for transfers between devices, side_by_side(): whole, at, outs = (lax.all_gather(both, axis, axis=dim, tiled=True), 0, [])  138 us
    all_to_all x1, blocking collectives, gather_over(): blocks = lax.all_to_all(blocks, name, split_axis=0, concat_axis=0)  64.7 us
    all_gather x5, blocking collectives, all_in_one(): both, at, found = (lax.all_gather(jnp.concatenate(lines), axis), 0, {})  50.5 us
    dynamic_slice x32, local copies, waits for them, and re-layouts, one_block(): value_part = lax.dynamic_slice_in_dim(value_rows, start_row, block_rows, 0)  34.3 us
    dot_general x32, matrix products, attend_rows(): jnp.einsum('kgqr,rkd->kgqd', weights.astype(jnp.bfloat16), value_head_row...  30.3 us
    dot_general x32, matrix products, attend_rows(): jnp.einsum('qkgd,rkd->kgqr', query_heads, key_head_rows, preferred_elemen...  17.2 us
    reduce_sum x32, other arithmetic, attend_rows(): row_total = row_total * rescale + jnp.sum(weights, axis=-1)  16.7 us
    all_to_all x1, waiting for transfers between devices, sum_at_owner(): lax.all_to_all(pieces, axis, split_axis=0, concat_axis=0, tiled=True)  11.5 us
  transfers between devices with their start and end apart: 2, of which 2 were waited for; matrix products, arithmetic and copies ran while one was open for 1% of the time, Pallas kernels for 0%

profile of v1, /device:TPU:1, one launch (start us, length us, event | category | flops | bytes accessed | tf_op | source)
XLA Modules:
  0.0 440.8 jit_solution(16072850196109958602)
XLA Ops:
  10.7 1.1 copy.48
  13.5 137.8 %all-gather.12.cloned.1.call-done = bf16[16384,512]{0,1:T(8,128)(2,1)} async-done(((bf16[128,512]{0,1:T(8,128)(2,1)}), bf16[16384,512]{0,1:T(8,128)(2,1)}) %all-gather.12.cloned.1.call-update) | async-done | bytes 16777232 | tf_op jit(solution)/shard_map/all_gather | solution.py:23
  151.2 11.4 %fusion.75 = (bf16[16384,256]{0,1:T(8,128)(2,1)}, bf16[16384,256]{0,1:T(8,128)(2,1)}) fusion(bf16[16384,512]{0,1:T(8,128)(2,1)} %all-gather.12.cloned.1.call-done), kind=kLoop, calls=%fused_computation.156 | loop fusion | bytes 33554432 | tf_op jit(solution)/shard_map/slice | solution.py:25
  162.7 113.7 %while.18 = (s32[]{:T(128)}, f32[2,4,128]{2,1,0:T(4,128)S(1)}, f32[2,4,128]{2,1,0:T(4,128)S(1)}, f32[2,4,128,128]{3,2,1,0:T(8,128)S(1)}, s32[8]{0:T(128)S(1)}, /...) while((s32[]{:T(128)}, f32[2,4,128]{2,1,0:T(4,128)S(1)}, ...), condition=%wide.region_6.7_spmd.clone, body=%wide.region_2.6_spmd.clone.sunk | while | flops 275925120 | bytes 9515759 | solution.py:126
  163.1 1.1 constant_dynamic-slice_fusion.3
  166.6 1.1 constant_dynamic-slice_fusion.3
  170.2 1.1 constant_dynamic-slice_fusion.3
  173.7 1.1 constant_dynamic-slice_fusion.3
  177.3 1.1 constant_dynamic-slice_fusion.3
  180.8 1.1 constant_dynamic-slice_fusion.3
  184.4 1.1 constant_dynamic-slice_fusion.3
  187.9 1.1 constant_dynamic-slice_fusion.3
  195.0 1.1 constant_dynamic-slice_fusion.3
  198.6 1.1 constant_dynamic-slice_fusion.3
  202.1 1.1 constant_dynamic-slice_fusion.3
  205.7 1.1 constant_dynamic-slice_fusion.3
  209.3 1.1 constant_dynamic-slice_fusion.3
  212.8 1.1 constant_dynamic-slice_fusion.3
  216.4 1.1 constant_dynamic-slice_fusion.3
  219.9 1.1 constant_dynamic-slice_fusion.3
  223.5 1.1 constant_dynamic-slice_fusion.3
  227.0 1.1 constant_dynamic-slice_fusion.3
  230.6 1.1 constant_dynamic-slice_fusion.3
  234.1 1.1 constant_dynamic-slice_fusion.3
  241.2 1.1 constant_dynamic-slice_fusion.3
  244.8 1.1 constant_dynamic-slice_fusion.3
  248.3 1.1 constant_dynamic-slice_fusion.3
  251.9 1.1 constant_dynamic-slice_fusion.3
  255.5 1.1 constant_dynamic-slice_fusion.3
  259.0 1.1 constant_dynamic-slice_fusion.3
  262.6 1.1 constant_dynamic-slice_fusion.3
  266.1 1.1 constant_dynamic-slice_fusion.3
  269.7 1.1 constant_dynamic-slice_fusion.3
  273.2 1.1 constant_dynamic-slice_fusion.3
  277.6 4.6 %convolution_convert_fusion = bf16[4,4096]{1,0:T(4,128)(2,1)S(1)} fusion(bf16[1024,4096]{1,0:T(8,128)(2,1)} %param.21, bf16[4,1024]{1,0:T(4,128)(2,1)S(1)} %gather_fusion, pred[4]{0:T(512)(128)(4,1)S(1)} %compare_and_fusion.1), kind=kOutput, calls=%fused_computation.27 | convolution fusion | flops 33574912 | bytes 8429572 | tf_op jit(solution)/shard_map/dot_general | solution.py:178
  282.2 5.1 %all_to_all.21 = bf16[2,4,2048]{2,1,0:T(4,128)(2,1)S(1)} all-to-all(bf16[2,4,2048]{2,1,0:T(4,128)(2,1)S(1)} %bitcast.364), channel_id=1, replica_groups=mesh['ctx_0'=4,'ctx_1'=2,'ctx_2'=8,'ctx_3'=2,'head'=2] {'head'}, dimensions={0} | all-to-all | bytes 65536 | tf_op jit(solution)/shard_map/all_to_all | solution.py:37
  287.5 5.0 %all_to_all.22 = f32[2,1,4]{2,1,0:T(1,128)S(1)} all-to-all(f32[2,1,4]{2,1,0:T(1,128)S(1)} %broadcast_in_dim.94), channel_id=1, replica_groups=mesh['ctx_0'=4,'ctx_1'=2,'ctx_2'=8,'ctx_3'=2,'head'=2] {'head'}, dimensions={0} | all-to-all | bytes 64 | tf_op jit(solution)/shard_map/all_to_all | solution.py:43
  293.6 64.7 %all_to_all.23 = bf16[128,4,2048]{2,1,0:T(4,128)(2,1)S(1)} all-to-all(bf16[128,4,2048]{2,1,0:T(4,128)(2,1)S(1)} %stack.2), channel_id=1, replica_groups=mesh['ctx_0'=4,'ctx_1'=2,'ctx_2'=8,'ctx_3'=2,'head'=2] {'ctx_0','ctx_1',..., dimensions={0} | all-to-all | bytes 4194304 | tf_op jit(solution)/shard_map/all_to_all | solution.py:17
  358.3 2.1 reshape.1082
  360.4 5.1 %convolution_convert_fusion.1 = bf16[512,1002]{0,1:T(8,128)(2,1)S(1)} fusion(bf16[512,2048]{1,0:T(8,128)(2,1)} %reshape.1082, bf16[2048,1002]{0,1:T(8,128)(2,1)} %param.22), kind=kOutput, calls=%fused_computation.29 | convolution fusion | flops 2101859328 | bytes 7227392 | tf_op jit(solution)/shard_map/dot_general | solution.py:186
  365.6 1.2 reshape.1083
  366.8 3.6 all-to-all-start.3
  370.4 11.5 %all-to-all-done.3 = bf16[2,512,501]{1,2,0:T(8,128)(2,1)S(1)} async-done(((bf16[2,512,501]{1,2,0:T(8,128)(2,1)}), bf16[2,512,501]{1,2,0:T(8,128)(2,1)S(1)}, u32[]{:S(2)}, u32[]{:S(2)}) %all-to-all-start.3) | async-done | bytes 1026080 | tf_op jit(solution)/shard_map/all_to_all | solution.py:37
  382.5 11.5 %all-gather.5 = f32[4,3,512]{2,1,0:T(4,128)S(1)} all-gather(f32[1,3,512]{2,1,0:T(4,128)S(1)} %maximum_bitcast_fusion), channel_id=2, replica_groups=mesh['ctx_0'=4,'ctx_1'=2,'ctx_2'=8,'ctx_3'=2,'head'=2] {'ctx_0'}, dimensions={0}, use_global_device_ids=true | all-gather | bytes 30720 | tf_op jit(solution)/shard_map/all_gather | solution.py:61
  394.0 4.7 %all-gather.6 = f32[2,3,512]{2,1,0:T(4,128)S(1)} all-gather(f32[1,3,512]{2,1,0:T(4,128)S(1)} %maximum_bitcast_fusion.1), channel_id=3, replica_groups=mesh['ctx_0'=4,'ctx_1'=2,'ctx_2'=8,'ctx_3'=2,'head'=2] {'ctx_1'}, dimensions={0}, use_global_device_ids=true | all-gather | bytes 18432 | tf_op jit(solution)/shard_map/all_gather | solution.py:61
  398.8 18.5 %all-gather.7 = f32[8,3,512]{2,1,0:T(4,128)S(1)} all-gather(f32[1,3,512]{2,1,0:T(4,128)S(1)} %maximum_bitcast_fusion.2), channel_id=4, replica_groups=mesh['ctx_0'=4,'ctx_1'=2,'ctx_2'=8,'ctx_3'=2,'head'=2] {'ctx_2'}, dimensions={0}, use_global_device_ids=true | all-gather | bytes 55296 | tf_op jit(solution)/shard_map/all_gather | solution.py:61
  417.4 12.7 %all-gather.8 = f32[2,3,512]{2,1,0:T(4,128)S(1)} all-gather(f32[1,3,512]{2,1,0:T(4,128)S(1)} %maximum_bitcast_fusion.3), channel_id=5, replica_groups=mesh['ctx_0'=4,'ctx_1'=2,'ctx_2'=8,'ctx_3'=2,'head'=2] {'ctx_3'}, dimensions={0}, use_global_device_ids=true | all-gather | bytes 18432 | tf_op jit(solution)/shard_map/all_gather | solution.py:61
  430.1 3.2 all-gather.9
  (411 shorter events, 88.1 us)
Async XLA Ops:
  7.2 144.1 %all-gather.12.cloned.1.call-start = ((), (), s32[]{:S(2)}) async-start(), calls=%async_computation.4 | async-start | bytes 16908288 | tf_op jit(solution)/shard_map/all_gather | solution.py:23
  277.0 5.2 %copy-start = (bf16[128,1024]{1,0:T(8,128)(2,1)}, bf16[128,1024]{1,0:T(8,128)(2,1)S(1)}, u32[]{:S(2)}) copy-start(bf16[128,1024]{1,0:T(8,128)(2,1)S(1)} %convert_element_type.47) | copy-start | bytes 786436
  277.6 9.8 %copy-start.1 = (bf16[4,2048]{1,0:T(4,128)(2,1)S(1)}, bf16[4,2048]{1,0:T(4,128)(2,1)}, u32[]{:S(2)}) copy-start(bf16[4,2048]{1,0:T(4,128)(2,1)} %param.19) | copy-start | bytes 49156
  277.6 14.9 %copy-start.2 = (f32[2048]{0:T(1024)S(1)}, f32[2048]{0:T(1024)}, u32[]{:S(2)}) copy-start(f32[2048]{0:T(1024)} %param.20) | copy-start | bytes 24580
  365.6 4.8 %copy-start.5 = (s32[512]{0:T(512)S(1)}, s32[512]{0:T(512)}, u32[]{:S(2)}) copy-start(s32[512]{0:T(512)} %param.23) | copy-start | bytes 6148
  366.8 15.1 %all-to-all-start.3 = ((bf16[2,512,501]{1,2,0:T(8,128)(2,1)}), bf16[2,512,501]{1,2,0:T(8,128)(2,1)S(1)}, u32[]{:S(2)}, u32[]{:S(2)}) async-start(bf16[2,512,501]{1,2,0:T(8,128)(2,1)} %bitcast.7), calls=%async_computation.3 | async-start | bytes 2064384 | tf_op jit(solution)/shard_map/all_to_all | solution.py:37
  370.4 62.9 %copy-start.3 = (f32[512]{0:T(512)S(1)}, f32[512]{0:T(512)}, u32[]{:S(2)}) copy-start(f32[512]{0:T(512)} %param.25) | copy-start | bytes 6148
  370.4 62.9 %copy-start.4 = (f32[512]{0:T(512)S(1)}, f32[512]{0:T(512)}, u32[]{:S(2)}) copy-start(f32[512]{0:T(512)} %param.24) | copy-start | bytes 6148
Sparse Core Ops, SparseCore 0:
  12.3 138.8 all-gather.11
